TPU v7x, 128 devices: a whole 4x4x4 slice. The times are simulated.
128 devices in a mesh: seq: 32 (over y, z, core), dp: 4 (over x).
Axes of the slice: x: 4, y: 4, z: 4, core: 2. Of those that a mesh axis runs over, the one named last changes fastest.
Arguments:
- query_input: bfloat16 [4, 16384, 2048], P('dp', 'seq'), may hold values from -6 to 6
- key_input: bfloat16 [4, 16384, 2048], P('dp', 'seq'), may hold values from -6 to 6
- value_input: bfloat16 [4, 16384, 2048], P('dp', 'seq'), may hold values from -6 to 6
- grad_output: bfloat16 [4, 16384, 2048], P('dp', 'seq'), may hold values from -6 to 6
- out_weight: bfloat16 [2048, 2048], P(('seq', 'dp')), may hold values from -0.125 to 0.125
- norm_gain: float32 [2048], replicated, may hold values from 0.1 to 1.9
Outputs:
- result: bfloat16 [4, 16384, 2048], P('dp', 'seq')
- grad_query: bfloat16 [4, 16384, 2048], P('dp', 'seq')
- grad_key: bfloat16 [4, 16384, 2048], P('dp', 'seq')
- grad_value: bfloat16 [4, 16384, 2048], P('dp', 'seq')
- grad_weight: float32 [2048, 2048], P(('seq', 'dp'))
All inputs are finite; a program needn't handle non-finite values.
Results may differ from a plain program's by a relative error of at most 0.015.
Values may be sent and summed in bfloat16 or wider, within the bound.
No kernel may reach another device: no remote copies, remote signals or barrier semaphores. Data moves between devices by JAX's collectives and lax.ppermute only.
A program may use at most 192 MiB of HBM per device.

v0:
```python
import jax
import jax.numpy as jnp
from jax import lax
from jax.sharding import Mesh
from jax.sharding import PartitionSpec as P

HEADS = 16
HEAD_DIM = 128
BLOCK = 512
SEQ = ("seq_0", "seq_1", "seq_2")
SEQ_DP = ("seq_0", "seq_1", "seq_2", "dp")
epsilon = 1e-06


def filled_with(shard, identity):
    return jnp.zeros_like(shard) + jnp.asarray(identity, shard.dtype)


def entering(shard, axes, combine, identity, reverse):
    before = start = filled_with(shard, identity)
    total = shard
    for axis in reversed(axes):
        peers, index = (lax.axis_size(axis), lax.axis_index(axis))
        pieces = lax.all_gather(total, axis)
        inside, total = (start, start)
        for k in reversed(range(peers)) if reverse else range(peers):
            passed = k > index if reverse else k < index
            total = combine(total, pieces[k])
            inside = jnp.where(passed, total, inside)
        before = combine(inside, before)
    return before


def split_up(shard, dim, peers):
    shape = shard.shape
    blocks = shard.reshape(*shape[:dim], peers, shape[dim] // peers, *shape[dim + 1 :])
    return jnp.moveaxis(blocks, dim, 0)


def scatter_pairs(shard, chips, core, dim):
    sizes = (lax.axis_size(chips), lax.axis_size(core))
    blocks = split_up(shard, dim, sizes[0] * sizes[1])
    inside = blocks.shape[1:]
    blocks = blocks.reshape(*sizes, *inside).swapaxes(0, 1).reshape(-1, *inside)
    blocks = lax.psum_scatter(blocks, core, scatter_dimension=0, tiled=True)
    return lax.psum_scatter(blocks, chips, scatter_dimension=0, tiled=True)[0]


def sent_and_summed(shard, axis, dim):
    peers = lax.axis_size(axis)
    blocks = lax.all_to_all(split_up(shard, dim, peers), axis, 0, 0, tiled=True)
    return jnp.sum(blocks.astype(jnp.float32), axis=0)


def silu_slope(inputs):
    sigmoid_value = jax.nn.sigmoid(inputs)
    return sigmoid_value * (1.0 + inputs * (1.0 - sigmoid_value))


def add_states(earlier, following):
    return earlier + following


def causal_product(left, right):
    scores = jnp.einsum("ihd,jhd->hij", left, right, preferred_element_type=jnp.float32)
    length_now = left.shape[0]
    causal = jnp.arange(length_now)[:, None] >= jnp.arange(length_now)[None, :]
    return jnp.where(causal[None], scores, 0.0)


def product(form, left, right):
    return jnp.einsum(form, left, right, preferred_element_type=jnp.float32)


def forward_parts(query_block, key_block, value_block, state_low):
    score_block = causal_product(query_block, key_block).astype(jnp.bfloat16)
    inside = product("hij,jhe->ihe", score_block, value_block)
    carried = product("ihd,hde->ihe", query_block, state_low)
    return (inside + carried, score_block)


def forward_only(items):
    return forward_parts(*items)[0]


def backward_core(
    query_block, key_block, value_block, grad_block, state_low, later_low, score_block
):
    grad_scores = causal_product(grad_block, value_block).astype(jnp.bfloat16)
    grad_fq = product("hij,jhd->ihd", grad_scores, key_block) + product(
        "ihe,hde->ihd", grad_block, state_low
    )
    grad_fk = product("hij,ihd->jhd", grad_scores, query_block) + product(
        "jhe,hde->jhd", value_block, later_low
    )
    grad_fv = product("hij,ihe->jhe", score_block, grad_block) + product(
        "jhd,hde->jhe", key_block, later_low
    )
    return (grad_fq, grad_fk, grad_fv)


def backward_again(items):
    query_block, key_block = (items[0], items[1])
    score_block = causal_product(query_block, key_block).astype(jnp.bfloat16)
    return backward_core(*items + (score_block,))


def shards(query_input, key_input, value_input, grad_output, out_weight, norm_gain):
    tokens = query_input.shape[1]
    feature_count = query_input.shape[2]
    blocks = tokens // BLOCK
    query_raw = query_input[0].astype(jnp.float32)
    key_raw = key_input[0].astype(jnp.float32)
    feat_query = jax.nn.silu(query_raw).astype(jnp.bfloat16).reshape(blocks, BLOCK, HEADS, HEAD_DIM)
    feat_key = jax.nn.silu(key_raw).astype(jnp.bfloat16).reshape(blocks, BLOCK, HEADS, HEAD_DIM)
    value_blocks = value_input[0].reshape(blocks, BLOCK, HEADS, HEAD_DIM)
    zero_state = jnp.zeros((HEADS, HEAD_DIM, HEAD_DIM), jnp.float32)
    block_kv = product("bjhd,bjhe->bhde", feat_key, value_blocks)
    local_incl = jnp.cumsum(block_kv, axis=0)
    incoming = entering(local_incl[-1], SEQ, add_states, zero_state, False)
    prefix = (incoming[None] + (local_incl - block_kv)).astype(jnp.bfloat16)
    full_weight = lax.all_gather(out_weight, SEQ_DP, axis=0, tiled=True)
    attention = lax.map(forward_only, (feat_query, feat_key, value_blocks, prefix))
    attention = attention.reshape(tokens, feature_count)
    radius = jnp.sqrt(jnp.mean(attention * attention, axis=-1, keepdims=True) + epsilon)
    normed = attention / radius
    mixed = (normed * norm_gain).astype(jnp.bfloat16)
    result = jnp.dot(mixed, full_weight, preferred_element_type=jnp.float32).astype(jnp.bfloat16)
    grad_result = grad_output[0]
    grad_mixed = lax.dot_general(
        grad_result, full_weight, (((1,), (1,)), ((), ())), preferred_element_type=jnp.float32
    )
    grad_hat = grad_mixed * norm_gain
    grad_att = (grad_hat - normed * jnp.mean(grad_hat * normed, axis=-1, keepdims=True)) / radius
    grad_att = grad_att.astype(jnp.bfloat16).reshape(blocks, BLOCK, HEADS, HEAD_DIM)
    block_grad = product("bihd,bihe->bhde", feat_query, grad_att)
    suffix_incl = jnp.cumsum(block_grad[::-1], axis=0)[::-1]
    incoming_later = entering(suffix_incl[0], SEQ, add_states, zero_state, True)
    later = (incoming_later[None] + (suffix_incl - block_grad)).astype(jnp.bfloat16)
    grad_fq, grad_fk, grad_fv = lax.map(
        backward_again, (feat_query, feat_key, value_blocks, grad_att, prefix, later)
    )
    grad_query = (grad_fq.reshape(tokens, feature_count) * silu_slope(query_raw)).astype(
        jnp.bfloat16
    )
    grad_key = (grad_fk.reshape(tokens, feature_count) * silu_slope(key_raw)).astype(jnp.bfloat16)
    grad_value = grad_fv.reshape(tokens, feature_count).astype(jnp.bfloat16)
    partial_value = scatter_pairs(
        lax.dot_general(
            mixed, grad_result, (((0,), (0,)), ((), ())), preferred_element_type=jnp.float32
        ).astype(jnp.bfloat16),
        ("seq_0", "seq_1"),
        "seq_2",
        0,
    ).astype(jnp.float32)
    grad_weight = sent_and_summed(partial_value.astype(jnp.bfloat16), "dp", 0)
    return (result[None], grad_query[None], grad_key[None], grad_value[None], grad_weight)


def solution(mesh):
    torus = Mesh(mesh.devices.reshape(4, 4, 2, mesh.shape["dp"]), ("seq_0", "seq_1", "seq_2", "dp"))
    placed = (
        P("dp", SEQ, None),
        P("dp", SEQ, None),
        P("dp", SEQ, None),
        P("dp", SEQ, None),
        P(SEQ_DP, None),
        P(),
    )
    return jax.shard_map(
        shards,
        mesh=torus,
        in_specs=placed,
        out_specs=(
            P("dp", SEQ, None),
            P("dp", SEQ, None),
            P("dp", SEQ, None),
            P("dp", SEQ, None),
            P(SEQ_DP, None),
        ),
        check_vma=False,
    )
```

profile of v0, /device:TPU:2, one launch (start us, length us, event | category | flops | bytes accessed | tf_op | source)
XLA Modules:
  0.0 469.6 jit_solution(1941817382321238800)
XLA Ops:
  7.2 2.3 copy.88
  11.1 1.6 multiply_convert_fusion.2
  12.7 1.3 copy-done.9
  14.1 2.4 fusion.23
  16.5 15.8 %all-gather.18.cloned.1.call-done = f32[32,128,128]{2,1,0:T(8,128)} async-done(((f32[16,128,128]{2,1,0:T(8,128)}), f32[32,128,128]{2,1,0:T(8,128)}) %all-gather.18.cloned.1.call-update) | async-done | bytes 2097168 | tf_op jit(solution)/shard_map/all_gather | solution.py:24
  32.3 2.6 slice_add_fusion.13
  35.1 49.8 %all-gather.22.cloned.1.call-done = f32[64,128,128]{2,1,0:T(8,128)} async-done(((f32[16,128,128]{2,1,0:T(8,128)}), f32[64,128,128]{2,1,0:T(8,128)}) %all-gather.22.cloned.1.call-update) | async-done | bytes 4194320 | tf_op jit(solution)/shard_map/all_gather | solution.py:24
  84.9 3.4 fusion.36
  89.4 2.1 convert_bitcast_fusion.1
  92.6 1.6 multiply_convert_fusion.3
  94.2 1.3 copy-done.5
  95.5 2.5 select_convert_fusion.1
  98.0 3.4 copy-done.4
  101.5 4.9 %fusion.19 = f32[16,512,128]{1,2,0:T(8,128)} fusion(bf16[16,512,512]{2,1,0:T(8,128)(2,1)S(1)} %select_convert_fusion.1, bf16[512,16,128]{2,1,0:T(8,128)(2,1)S(1)} %bitcast.110), kind=kOutput, calls=%fused_computation.41 | convolution fusion | flops 1073741824 | bytes 14680064 | tf_op jit(solution)/shard_map/while/body/eval_jaxpr/hij,jhe->ihe/dot_general | solution.py:72
  106.4 30.5 %all-gather.12.cloned.1.call-done = f32[4,16,128,128]{3,2,1,0:T(8,128)} async-done(((f32[1,16,128,128]{3,2,1,0:T(8,128)}), f32[4,16,128,128]{3,2,1,0:T(8,128)}) %all-gather.12.cloned.1.call-update) | async-done | bytes 4194320 | tf_op jit(solution)/shard_map/all_gather | solution.py:24
  136.9 5.8 %fusion.35 = bf16[16,128,128]{2,1,0:T(8,128)(2,1)S(1)} fusion(f32[4,16,128,128]{3,2,1,0:T(8,128)} %all-gather.12.cloned.1.call-done, f32[16,128,128]{2,1,0:T(8,128)} %fusion.23, f32[64,128,128]{2,1,0:T(8,128)} %all-gather.22.cloned.1.call-done, f32[32,128,128]{2,1,0:T(8,128)} %all-gather.18.cloned.1.call-done, pred[]{:T(512)S(6)} %gt.35, pred[]{:T(512)S(6)} %gt.36, ...), kind=kLoop, calls=%fused_computation.65 | loop fusion | flops 5767168 | bytes 12058634 | tf_op jit(solution)/shard_map/convert_element_type | solution.py:121
  143.1 2.8 multiply_reduce_fusion.1
  145.8 5.6 %copy.64 = f32[512,2048]{1,0:T(8,128)} copy(f32[512,2048]{0,1:T(8,128)} %bitcast.106) | data formatting | bytes 8388608 | tf_op jit(solution)/shard_map/reshape | solution.py:124
  151.4 57.2 %all-gather.14.cloned.1.call-done = bf16[2048,2048]{1,0:T(8,128)(2,1)} async-done(((bf16[16,2048]{1,0:T(8,128)(2,1)}), bf16[2048,2048]{1,0:T(8,128)(2,1)}) %all-gather.14.cloned.1.call-update) | async-done | bytes 8388624 | tf_op jit(solution)/shard_map/all_gather | solution.py:122
  208.7 9.3 %multiply_reduce_fusion = (f32[512]{0:T(512)S(1)}, f32[512,2048]{1,0:T(8,128)S(1)}) fusion(f32[2048]{0:T(1024)S(1)} %copy-done.24, f32[512,2048]{1,0:T(8,128)} %copy.64, f32[512]{0:T(512)S(1)} %add_sqrt_fusion, bf16[2048,2048]{1,0:T(8,128)(2,1)} %all-gather.14.cloned.1.call-done, bf16[1,512,2048]{2,1,0:T(8,128)(2,1)S(1)} %copy-done), kind=kOutput, calls=%fused_computation.27 | convolution fusion | flops 4299161088 | bytes 18886656 | tf_op jit(solution)/shard_map/dot_general | solution.py:130
  218.0 2.2 divide_convert_fusion
  220.2 3.9 copy.85
  224.1 4.0 fusion.39
  228.2 12.2 %all-gather.20.cloned.1.call-done = f32[32,128,128]{2,1,0:T(8,128)} async-done(((f32[16,128,128]{2,1,0:T(8,128)}), f32[32,128,128]{2,1,0:T(8,128)}) %all-gather.20.cloned.1.call-update) | async-done | bytes 2097168 | tf_op jit(solution)/shard_map/all_gather | solution.py:24
  240.3 2.7 slice_add_fusion.6
  243.1 2.6 multiply_convert_fusion
  245.7 6.8 %convolution_convert_fusion = bf16[2048,2048]{1,0:T(8,128)(2,1)} fusion(bf16[512,2048]{0,1:T(8,128)(2,1)S(1)} %bitcast.118, bf16[1,512,2048]{2,1,0:T(8,128)(2,1)S(1)} %copy-done), kind=kOutput, calls=%fused_computation.2 | convolution fusion | flops 4299161600 | bytes 12582912 | tf_op jit(solution)/shard_map/dot_general | solution.py:149
  252.5 9.0 %copy.77 = bf16[16,2,64,2048]{3,2,0,1:T(8,128)(2,1)} copy(bf16[16,2,64,2048]{3,2,1,0:T(8,128)(2,1)} %bitcast.117) | data formatting | bytes 16777216 | tf_op jit(solution)/shard_map/reshape;reshape | solution.py:44
  261.6 31.3 %all-gather.24.cloned.1.call-done = f32[64,128,128]{2,1,0:T(8,128)} async-done(((f32[16,128,128]{2,1,0:T(8,128)}), f32[64,128,128]{2,1,0:T(8,128)}) %all-gather.24.cloned.1.call-update) | async-done | bytes 4194320 | tf_op jit(solution)/shard_map/all_gather | solution.py:24
  292.9 3.5 fusion.30
  296.4 18.4 %reduce-scatter.5.cloned.1.call-done = bf16[16,64,2048]{2,1,0:T(8,128)(2,1)} async-done(((bf16[32,64,2048]{2,1,0:T(8,128)(2,1)}), bf16[16,64,2048]{2,1,0:T(8,128)(2,1)}) %reduce-scatter.5.cloned.1.call-update) | async-done | bytes 4194320 | tf_op jit(solution)/shard_map/reduce_scatter | solution.py:45
  314.8 4.6 select_convert_fusion
  319.5 4.9 %fusion.37 = f32[16,128,512]{2,1,0:T(8,128)} fusion(bf16[512,16,128]{2,0,1:T(8,128)(2,1)S(1)} %copy-done.11, bf16[16,512,512]{2,1,0:T(8,128)(2,1)S(1)} %select_convert_fusion), kind=kOutput, calls=%fused_computation.81 | convolution fusion | flops 1073741824 | bytes 14680064 | tf_op jit(solution)/shard_map/while/body/eval_jaxpr/hij,jhd->ihd/dot_general | solution.py:72
  324.3 4.9 %convolution_add_fusion.1 = f32[16,128,512]{2,1,0:T(8,128)} fusion(f32[16,128,512]{2,1,0:T(8,128)} %fusion.37, bf16[16,128,128]{2,1,0:T(8,128)(2,1)S(1)} %fusion.35, bf16[512,16,128]{0,2,1:T(8,128)(2,1)S(1)} %bitcast.105), kind=kOutput, calls=%fused_computation.35 | convolution fusion | flops 269484032 | bytes 11010048 | tf_op jit(solution)/shard_map/while/body/eval_jaxpr/ihe,hde->ihd/dot_general | solution.py:72
  329.2 5.8 %copy.69 = f32[1,512,2048]{2,1,0:T(8,128)} copy(f32[1,512,2048]{1,2,0:T(8,128)} %bitcast.113) | data formatting | bytes 8388608 | tf_op jit(solution)/shard_map/reshape | solution.py:143
  335.0 7.7 %fusion.40 = f32[16,128,512]{2,1,0:T(8,128)} fusion(bf16[512,16,128]{0,2,1:T(8,128)(2,1)} %bitcast.103, bf16[16,512,512]{2,1,0:T(8,128)(2,1)} %copy-done.4), kind=kOutput, calls=%fused_computation.84 | convolution fusion | flops 1073741824 | bytes 14680064 | tf_op jit(solution)/shard_map/while/body/eval_jaxpr/hij,ihe->jhe/dot_general | solution.py:72
  343.7 3.6 fusion.38
  347.3 1.9 slice-done.1
  349.2 5.8 %fusion.14 = bf16[1,512,2048]{2,1,0:T(8,128)(2,1)} fusion(bf16[2048,2048]{1,0:T(8,128)(2,1)S(1)} %bitcast.123, f32[2048]{0:T(1024)S(1)} %copy-done.24, f32[512,2048]{1,0:T(8,128)S(1)} %copy-done.18, f32[512]{0:T(512)S(1)} %add_sqrt_fusion), kind=kOutput, calls=%fused_computation.33 | convolution fusion | flops 4299161600 | bytes 14690304 | tf_op jit(solution)/shard_map/dot_general | solution.py:128
  355.0 11.0 %all-gather.16.cloned.1.call-done = f32[4,16,128,128]{3,2,1,0:T(8,128)} async-done(((f32[1,16,128,128]{3,2,1,0:T(8,128)}), f32[4,16,128,128]{3,2,1,0:T(8,128)}) %all-gather.16.cloned.1.call-update) | async-done | bytes 4194320 | tf_op jit(solution)/shard_map/all_gather | solution.py:24
  365.9 5.5 %fusion.29 = bf16[16,128,128]{2,1,0:T(8,128)(2,1)S(1)} fusion(f32[4,16,128,128]{3,2,1,0:T(8,128)} %all-gather.16.cloned.1.call-done, f32[16,128,128]{2,1,0:T(8,128)S(1)} %copy-done.19, f32[64,128,128]{2,1,0:T(8,128)} %all-gather.24.cloned.1.call-done, f32[32,128,128]{2,1,0:T(8,128)} %all-gather.20.cloned.1.call-done, pred[]{:T(512)S(6)} %lt.37, pred[]{:T(512)S(6)} %lt.38, ...), kind=kLoop, calls=%fused_computation.52 | loop fusion | flops 5767168 | bytes 12058634 | tf_op jit(solution)/shard_map/convert_element_type | solution.py:139
  371.5 3.3 convolution_add_fusion
  374.8 5.5 %copy.74 = f32[1,512,2048]{2,1,0:T(8,128)} copy(f32[1,512,2048]{1,2,0:T(8,128)} %bitcast.114) | data formatting | bytes 8388608 | tf_op jit(solution)/shard_map/reshape | solution.py:146
  380.4 7.3 %fusion.6 = (bf16[1,512,2048]{2,1,0:T(8,128)(2,1)}, bf16[1,512,2048]{2,1,0:T(8,128)(2,1)}) fusion(f32[1,512,2048]{2,1,0:T(8,128)} %copy.69, bf16[1,512,2048]{2,1,0:T(8,128)(2,1)} %param.6, f32[1,512,2048]{2,1,0:T(8,128)} %copy.74, bf16[1,512,2048]{2,1,0:T(8,128)(2,1)S(1)} %copy-done.21), kind=kLoop, calls=%fused_computation.15 | loop fusion | flops 20971520 | bytes 16777216 | tf_op jit(solution)/shard_map/convert_element_type | solution.py:143
  387.6 60.7 %reduce-scatter.7.cloned.1.call-done = bf16[1,64,2048]{2,1,0:T(8,128)(2,1)} async-done(((bf16[16,64,2048]{2,1,0:T(8,128)(2,1)}), bf16[1,64,2048]{2,1,0:T(8,128)(2,1)}) %reduce-scatter.7.cloned.1.call-update) | async-done | bytes 262160
  448.3 4.8 %all-to-all-start = ((bf16[4,16,2048]{2,1,0:T(8,128)(2,1)}), bf16[4,16,2048]{2,1,0:T(8,128)(2,1)S(1)}, u32[]{:S(2)}, u32[]{:S(2)}) async-start(bf16[4,16,2048]{2,1,0:T(8,128)(2,1)} %bitcast.120), calls=%async_computation.1 | async-start | bytes 524288 | tf_op jit(solution)/shard_map/all_to_all | solution.py:51
  453.1 5.1 %add_convert_fusion = bf16[16,128,512]{2,1,0:T(8,128)(2,1)} fusion(f32[16,128,512]{2,1,0:T(8,128)} %fusion.40, bf16[16,128,128]{2,1,0:T(8,128)(2,1)S(1)} %copy-done.23, bf16[512,16,128]{2,0,1:T(8,128)(2,1)} %copy-done.9), kind=kOutput, calls=%fused_computation.25 | convolution fusion | flops 270532608 | bytes 8912896 | tf_op jit(solution)/shard_map/while/body/eval_jaxpr/jhd,hde->jhe/dot_general | solution.py:72
  458.2 3.9 copy.78
  (77 shorter events, 6.1 us)
Async XLA Ops:
  7.2 201.5 %copy-start = (bf16[1,512,2048]{2,1,0:T(8,128)(2,1)S(1)}, bf16[1,512,2048]{2,1,0:T(8,128)(2,1)}, u32[]{:S(2)}) copy-start(bf16[1,512,2048]{2,1,0:T(8,128)(2,1)} %param.9) | copy-start | bytes 6291460
  7.2 25.2 %all-gather.18.cloned.1.call-start = ((), (), s32[]{:S(2)}) async-start(), calls=%async_computation.7 | async-start | bytes 3145728 | tf_op jit(solution)/shard_map/all_gather | solution.py:24
  7.2 2.4 copy-start.20
  9.6 3.1 copy-start.12
  12.7 1.3 copy-start.9
  16.5 68.4 %all-gather.22.cloned.1.call-start = ((), (), s32[]{:S(2)}) async-start(), calls=%async_computation.9 | async-start | bytes 5242880 | tf_op jit(solution)/shard_map/all_gather | solution.py:24
  35.0 101.9 %all-gather.12.cloned.1.call-start = ((), (), s32[]{:S(2)}) async-start(), calls=%async_computation.3 | async-start | bytes 5242880 | tf_op jit(solution)/shard_map/all_gather | solution.py:24
  88.3 120.4 %all-gather.14.cloned.1.call-start = ((), (), s32[]{:S(2)}) async-start(), calls=%async_computation.4 | async-start | bytes 8454144 | tf_op jit(solution)/shard_map/all_gather | solution.py:122
  88.9 151.4 %all-gather.20.cloned.1.call-start = ((), (), s32[]{:S(2)}) async-start(), calls=%async_computation.8 | async-start | bytes 3145728 | tf_op jit(solution)/shard_map/all_gather | solution.py:24
  92.5 3.1 copy-start.10
  94.2 1.3 copy-start.5
  95.5 5.9 %copy-start.13 = (bf16[64,8,16,128]{3,2,1,0:T(8,128)(2,1)S(1)}, bf16[64,8,16,128]{3,2,1,0:T(8,128)(2,1)}, u32[]{:S(2)}) copy-start(bf16[64,8,16,128]{3,2,1,0:T(8,128)(2,1)} %copy-done.12) | copy-start | bytes 6291460
  98.0 3.5 copy-start.4
  136.9 5.9 %copy-start.6 = (bf16[512,16,128]{2,0,1:T(8,128)(2,1)S(1)}, bf16[512,16,128]{2,0,1:T(8,128)(2,1)}, u32[]{:S(2)}) copy-start(bf16[512,16,128]{2,0,1:T(8,128)(2,1)} %copy-done.5) | copy-start | bytes 6291460
  136.9 6.2 %copy-start.16 = (f32[16,512,128]{1,2,0:T(8,128)S(1)}, f32[16,512,128]{1,2,0:T(8,128)}, u32[]{:S(2)}) copy-start(f32[16,512,128]{1,2,0:T(8,128)} %fusion.19) | copy-start | bytes 12582916
  145.8 62.8 %copy-start.24 = (f32[2048]{0:T(1024)S(1)}, f32[2048]{0:T(1024)}, u32[]{:S(2)}) copy-start(f32[2048]{0:T(1024)} %param.11) | copy-start | bytes 24580
  208.7 9.3 %copy-start.17 = (f32[512,2048]{1,0:T(8,128)S(1)}, f32[512,2048]{1,0:T(8,128)}, u32[]{:S(2)}) copy-start(f32[512,2048]{1,0:T(8,128)} %copy.64) | copy-start | bytes 12582916
  228.1 64.7 %all-gather.24.cloned.1.call-start = ((), (), s32[]{:S(2)}) async-start(), calls=%async_computation.10 | async-start | bytes 5242880 | tf_op jit(solution)/shard_map/all_gather | solution.py:24
  243.0 71.7 %reduce-scatter.5.cloned.1.call-start = ((), (), s32[]{:S(2)}) async-start(), calls=%async_computation.6 | async-start | bytes 12582912 | tf_op jit(solution)/shard_map/reduce_scatter | solution.py:45
  261.5 53.3 %copy-start.8 = (bf16[512,2048]{0,1:T(8,128)(2,1)S(1)}, bf16[512,2048]{0,1:T(8,128)(2,1)}, u32[]{:S(2)}) copy-start(bf16[512,2048]{0,1:T(8,128)(2,1)} %copy.85) | copy-start | bytes 6291460
  261.5 104.4 %all-gather.16.cloned.1.call-start = ((), (), s32[]{:S(2)}) async-start(), calls=%async_computation.5 | async-start | bytes 5242880 | tf_op jit(solution)/shard_map/all_gather | solution.py:24
  296.4 152.0 %reduce-scatter.7.cloned.1.call-start = ((), (), s32[]{:S(2)}) async-start(), calls=%async_computation.11 | async-start | bytes 4456448
  314.8 4.6 copy-start.11
  319.4 4.9 %copy-start.2 = (bf16[16,512,512]{2,1,0:T(8,128)(2,1)}, bf16[16,512,512]{2,1,0:T(8,128)(2,1)S(1)}, u32[]{:S(2)}) copy-start(bf16[16,512,512]{2,1,0:T(8,128)(2,1)S(1)} %select_convert_fusion) | copy-start | bytes 25165828
  335.0 7.7 %copy-start.3 = (bf16[16,512,512]{2,1,0:T(8,128)(2,1)S(1)}, bf16[16,512,512]{2,1,0:T(8,128)(2,1)}, u32[]{:S(2)}) copy-start(bf16[16,512,512]{2,1,0:T(8,128)(2,1)} %copy-done.2) | copy-start | bytes 25165828
  335.0 8.7 %copy-start.7 = (bf16[512,16,128]{2,0,1:T(8,128)(2,1)S(1)}, bf16[512,16,128]{2,0,1:T(8,128)(2,1)}, u32[]{:S(2)}) copy-start(bf16[512,16,128]{2,0,1:T(8,128)(2,1)} %copy-done.5) | copy-start | bytes 6291460
  335.0 12.3 %slice-start = ((s8[8388608]{0:T(1024)(128)(4,1)}), s8[4194304]{0:T(1024)(128)(4,1)S(1)}, s32[]{:S(2)}) async-start(s8[8388608]{0:T(1024)(128)(4,1)} %bitcast.122), calls=%async_computation.12 | async-start | bytes 8388608
  343.7 3.6 copy-start.18
  343.7 5.5 %slice-start.1 = ((s8[8388608]{0:T(1024)(128)(4,1)}), s8[4194304]{0:T(1024)(128)(4,1)S(1)}, s32[]{:S(2)}) async-start(s8[8388608]{0:T(1024)(128)(4,1)} %bitcast.122), calls=%async_computation.13 | async-start | bytes 8388608
  349.2 16.8 %copy-start.19 = (f32[16,128,128]{2,1,0:T(8,128)S(1)}, f32[16,128,128]{2,1,0:T(8,128)}, u32[]{:S(2)}) copy-start(f32[16,128,128]{2,1,0:T(8,128)} %fusion.39) | copy-start | bytes 3145732
  355.0 16.5 %copy-start.14 = (bf16[64,8,16,128]{3,2,1,0:T(8,128)(2,1)S(1)}, bf16[64,8,16,128]{3,2,1,0:T(8,128)(2,1)}, u32[]{:S(2)}) copy-start(bf16[64,8,16,128]{3,2,1,0:T(8,128)(2,1)} %copy-done.12) | copy-start | bytes 6291460
  365.9 5.5 %copy-start.15 = (f32[16,128,512]{2,1,0:T(8,128)S(1)}, f32[16,128,512]{2,1,0:T(8,128)}, u32[]{:S(2)}) copy-start(f32[16,128,512]{2,1,0:T(8,128)} %fusion.38) | copy-start | bytes 12582916
  371.5 3.3 copy-start.22
  374.8 5.5 %copy-start.21 = (bf16[1,512,2048]{2,1,0:T(8,128)(2,1)S(1)}, bf16[1,512,2048]{2,1,0:T(8,128)(2,1)}, u32[]{:S(2)}) copy-start(bf16[1,512,2048]{2,1,0:T(8,128)(2,1)} %param.7) | copy-start | bytes 6291460
  380.3 72.8 %copy-start.23 = (bf16[16,128,128]{2,1,0:T(8,128)(2,1)S(1)}, bf16[16,128,128]{2,1,0:T(8,128)(2,1)}, u32[]{:S(2)}) copy-start(bf16[16,128,128]{2,1,0:T(8,128)(2,1)} %copy-done.22) | copy-start | bytes 1572868
  448.3 13.8 %all-to-all-start = ((bf16[4,16,2048]{2,1,0:T(8,128)(2,1)}), bf16[4,16,2048]{2,1,0:T(8,128)(2,1)S(1)}, u32[]{:S(2)}, u32[]{:S(2)}) async-start(bf16[4,16,2048]{2,1,0:T(8,128)(2,1)} %bitcast.120), calls=%async_computation.1 | async-start | bytes 524288 | tf_op jit(solution)/shard_map/all_to_all | solution.py:51
  453.1 9.7 %copy-start.1 = (bf16[1,512,2048]{2,1,0:T(8,128)(2,1)S(1)}, bf16[1,512,2048]{2,1,0:T(8,128)(2,1)}, u32[]{:S(2)}) copy-start(bf16[1,512,2048]{2,1,0:T(8,128)(2,1)} %param.9) | copy-start | bytes 6291460
Sparse Core Ops, SparseCore 0:
  16.6 15.7 all-gather.17
  35.1 49.6 all-gather.21
  88.4 48.3 all-gather.11
  139.9 68.7 all-gather.13
  228.2 12.0 all-gather.19
  243.2 49.6 all-gather.23
  295.3 19.4 reduce-scatter.4
  316.4 49.4 all-gather.15
  369.3 78.9 reduce-scatter.6
where the time goes:
time: 475 us; the launch traced here: 470 us
  waiting for transfers between devices  287 us (60%)
  matrix products  72.4 us (15%)
  local copies, waits for them, and re-layouts  47.3 us (10%)
  other arithmetic  42.3 us (9%)
  between operations  14.4 us (3%)
  starting transfers between devices  5.63 us (1%)
    all_gather x6, waiting for transfers between devices, entering(): pieces = lax.all_gather(total, axis)  151 us
    unnamed x10, waiting for transfers between devices  61.4 us
    all_gather x1, waiting for transfers between devices, shards(): full_weight = lax.all_gather(out_weight, SEQ_DP, axis=0, tiled=True)  57.2 us
    dot_general x10, matrix products, product(): return jnp.einsum(form, left, right, preferred_element_type=jnp.float32)  43.4 us
    reduce_scatter x1, waiting for transfers between devices, scatter_pairs(): blocks = lax.psum_scatter(blocks, core, scatter_dimension=0, tiled=True)  18.4 us
    unnamed x58, local copies, waits for them, and re-layouts  17.6 us
    add x4, other arithmetic, add_states(): return earlier + following  12.2 us
  transfers between devices with their start and end apart: 10, of which 9 were waited for; matrix products, arithmetic and copies ran while one was open for 25% of the time, Pallas kernels for 0%

commit v1 on v0

--- a/solution.py
+++ b/solution.py
@@ -119,7 +119,9 @@
     local_incl = jnp.cumsum(block_kv, axis=0)
     incoming = entering(local_incl[-1], SEQ, add_states, zero_state, False)
     prefix = (incoming[None] + (local_incl - block_kv)).astype(jnp.bfloat16)
-    full_weight = lax.all_gather(out_weight, SEQ_DP, axis=0, tiled=True)
+    full_weight = jnp.concatenate(
+        lax.all_to_all(jnp.stack([out_weight] * lax.axis_size(SEQ_DP)), SEQ_DP, 0, 0), axis=0
+    )
     attention = lax.map(forward_only, (feat_query, feat_key, value_blocks, prefix))
     attention = attention.reshape(tokens, feature_count)
     radius = jnp.sqrt(jnp.mean(attention * attention, axis=-1, keepdims=True) + epsilon)

time: 475 us -> 512 us (1.078)
  waiting for transfers between devices: 287 us -> 308 us
  starting transfers between devices: 5.63 us -> 15.5 us
    all_gather x6, waiting for transfers between devices: 151 us -> 229 us  [entering(): pieces = lax.all_gather(total, axis)]
    all_gather x1 -> x0, waiting for transfers between devices: 57.2 us -> none  [shards(): full_weight = lax.all_gather(out_weight, SEQ_DP, axis=0, tiled=True)]
    all_to_all x0 -> x1, starting transfers between devices: none -> 9.89 us  [shards(): lax.all_to_all(jnp.stack([out_weight] * lax.axis_size(SEQ_DP)), SEQ_DP, 0...]
    unnamed x10 -> x9, waiting for transfers between devices: 61.4 us -> 60.8 us
  transfers between devices with their start and end apart: 10 -> 10, of which waited for: 9 -> 8; matrix products, arithmetic and copies ran while one was open for 25% -> 25% of each run, Pallas kernels for 0% -> 0%
where the time goes in v1:
time: 512 us; the launch traced here: 506 us
  waiting for transfers between devices  308 us (60%)
  matrix products  75.8 us (15%)
  local copies, waits for them, and re-layouts  50 us (10%)
  other arithmetic  42.3 us (8%)
  starting transfers between devices  15.5 us (3%)
  between operations  14.7 us (3%)
    all_gather x6, waiting for transfers between devices, entering(): pieces = lax.all_gather(total, axis)  229 us
    unnamed x9, waiting for transfers between devices  60.8 us
    dot_general x10, matrix products, product(): return jnp.einsum(form, left, right, preferred_element_type=jnp.float32)  43.5 us
    reduce_scatter x1, waiting for transfers between devices, scatter_pairs(): blocks = lax.psum_scatter(blocks, core, scatter_dimension=0, tiled=True)  18.2 us
    unnamed x58, local copies, waits for them, and re-layouts  15.8 us
    add x4, other arithmetic, add_states(): return earlier + following  12.2 us
  transfers between devices with their start and end apart: 10, of which 8 were waited for; matrix products, arithmetic and copies ran while one was open for 25% of the time, Pallas kernels for 0%

profile of v1, /device:TPU:2, one launch (start us, length us, event | category | flops | bytes accessed | tf_op | source)
XLA Modules:
  0.0 506.0 jit_solution(9683974608476083310)
XLA Ops:
  7.2 2.3 copy.88
  11.1 1.6 multiply_convert_fusion.1
  12.7 1.3 copy-done.9
  14.1 2.4 fusion.22
  16.6 15.8 %all-gather.15.cloned.1.call-done = f32[32,128,128]{2,1,0:T(8,128)} async-done(((f32[16,128,128]{2,1,0:T(8,128)}), f32[32,128,128]{2,1,0:T(8,128)}) %all-gather.15.cloned.1.call-update) | async-done | bytes 2097168 | tf_op jit(solution)/shard_map/all_gather | solution.py:24
  32.4 2.6 slice_add_fusion.13
  35.1 4.3 stack.2
  39.4 9.9 %all-to-all-start = ((bf16[128,16,2048]{2,1,0:T(8,128)(2,1)}), bf16[128,16,2048]{2,1,0:T(8,128)(2,1)}, u32[]{:S(2)}, u32[]{:S(2)}) async-start(bf16[128,16,2048]{2,1,0:T(8,128)(2,1)} %stack.2), calls=%async_computation | async-start | bytes 16777216 | tf_op jit(solution)/shard_map/all_to_all | solution.py:123
  49.4 126.8 %all-gather.19.cloned.1.call-done = f32[64,128,128]{2,1,0:T(8,128)} async-done(((f32[16,128,128]{2,1,0:T(8,128)}), f32[64,128,128]{2,1,0:T(8,128)}) %all-gather.19.cloned.1.call-update) | async-done | bytes 4194320 | tf_op jit(solution)/shard_map/all_gather | solution.py:24
  176.2 3.4 fusion.35
  180.2 2.1 convert_bitcast_fusion.1
  183.4 1.6 multiply_convert_fusion.2
  185.0 1.3 copy-done.5
  186.3 2.5 select_convert_fusion.1
  188.8 3.6 copy-done.4
  192.4 5.0 fusion.18
  197.3 31.4 %all-gather.11.cloned.1.call-done = f32[4,16,128,128]{3,2,1,0:T(8,128)} async-done(((f32[1,16,128,128]{3,2,1,0:T(8,128)}), f32[4,16,128,128]{3,2,1,0:T(8,128)}) %all-gather.11.cloned.1.call-update) | async-done | bytes 4194320 | tf_op jit(solution)/shard_map/all_gather | solution.py:24
  228.7 5.8 %fusion.34 = bf16[16,128,128]{2,1,0:T(8,128)(2,1)S(1)} fusion(f32[4,16,128,128]{3,2,1,0:T(8,128)} %all-gather.11.cloned.1.call-done, f32[16,128,128]{2,1,0:T(8,128)} %fusion.22, f32[64,128,128]{2,1,0:T(8,128)} %all-gather.19.cloned.1.call-done, f32[32,128,128]{2,1,0:T(8,128)} %all-gather.15.cloned.1.call-done, pred[]{:T(512)S(6)} %gt.35, pred[]{:T(512)S(6)} %gt.36, ...), kind=kLoop, calls=%fused_computation.63 | loop fusion | flops 5767168 | bytes 12058634 | tf_op jit(solution)/shard_map/convert_element_type | solution.py:121
  234.9 2.8 multiply_reduce_fusion.1
  237.7 5.5 %copy.64 = f32[512,2048]{1,0:T(8,128)} copy(f32[512,2048]{0,1:T(8,128)} %bitcast.108) | data formatting | bytes 8388608 | tf_op jit(solution)/shard_map/reshape | solution.py:126
  243.3 9.3 %multiply_reduce_fusion = (f32[512]{0:T(512)S(1)}, f32[512,2048]{1,0:T(8,128)S(1)}) fusion(f32[2048]{0:T(1024)S(1)} %copy-done.26, f32[512,2048]{1,0:T(8,128)} %copy.64, f32[512]{0:T(512)S(1)} %add_sqrt_fusion, bf16[2048,2048]{1,0:T(8,128)(2,1)} %bitcast.8, bf16[1,512,2048]{2,1,0:T(8,128)(2,1)S(1)} %copy-done), kind=kOutput, calls=%fused_computation.26 | convolution fusion | flops 4299161088 | bytes 18886656 | tf_op jit(solution)/shard_map/dot_general | solution.py:132
  252.6 2.2 divide_convert_fusion
  254.9 3.9 copy.85
  258.8 4.0 fusion.38
  262.8 13.8 %all-gather.17.cloned.1.call-done = f32[32,128,128]{2,1,0:T(8,128)} async-done(((f32[16,128,128]{2,1,0:T(8,128)}), f32[32,128,128]{2,1,0:T(8,128)}) %all-gather.17.cloned.1.call-update) | async-done | bytes 2097168 | tf_op jit(solution)/shard_map/all_gather | solution.py:24
  276.6 2.7 slice_add_fusion.6
  279.3 2.6 multiply_convert_fusion
  282.0 6.8 %convolution_convert_fusion = bf16[2048,2048]{1,0:T(8,128)(2,1)} fusion(bf16[512,2048]{0,1:T(8,128)(2,1)S(1)} %bitcast.120, bf16[1,512,2048]{2,1,0:T(8,128)(2,1)S(1)} %copy-done), kind=kOutput, calls=%fused_computation.2 | convolution fusion | flops 4299161600 | bytes 12582912 | tf_op jit(solution)/shard_map/dot_general | solution.py:151
  288.7 9.0 %copy.77 = bf16[16,2,64,2048]{3,2,0,1:T(8,128)(2,1)} copy(bf16[16,2,64,2048]{3,2,1,0:T(8,128)(2,1)} %bitcast.119) | data formatting | bytes 16777216 | tf_op jit(solution)/shard_map/reshape;reshape | solution.py:44
  297.8 31.3 %all-gather.21.cloned.1.call-done = f32[64,128,128]{2,1,0:T(8,128)} async-done(((f32[16,128,128]{2,1,0:T(8,128)}), f32[64,128,128]{2,1,0:T(8,128)}) %all-gather.21.cloned.1.call-update) | async-done | bytes 4194320 | tf_op jit(solution)/shard_map/all_gather | solution.py:24
  329.1 3.4 fusion.29
  332.7 18.2 %reduce-scatter.5.cloned.1.call-done = bf16[16,64,2048]{2,1,0:T(8,128)(2,1)} async-done(((bf16[32,64,2048]{2,1,0:T(8,128)(2,1)}), bf16[16,64,2048]{2,1,0:T(8,128)(2,1)}) %reduce-scatter.5.cloned.1.call-update) | async-done | bytes 4194320 | tf_op jit(solution)/shard_map/reduce_scatter | solution.py:45
  350.9 4.6 select_convert_fusion
  355.6 4.9 fusion.36
  360.4 4.9 convolution_add_fusion.1
  365.4 5.8 %copy.69 = f32[1,512,2048]{2,1,0:T(8,128)} copy(f32[1,512,2048]{1,2,0:T(8,128)} %bitcast.115) | data formatting | bytes 8388608 | tf_op jit(solution)/shard_map/reshape | solution.py:145
  371.1 7.7 %fusion.39 = f32[16,128,512]{2,1,0:T(8,128)} fusion(bf16[512,16,128]{0,2,1:T(8,128)(2,1)} %bitcast.105, bf16[16,512,512]{2,1,0:T(8,128)(2,1)} %copy-done.4), kind=kOutput, calls=%fused_computation.82 | convolution fusion | flops 1073741824 | bytes 14680064 | tf_op jit(solution)/shard_map/while/body/eval_jaxpr/hij,ihe->jhe/dot_general | solution.py:72
  379.8 3.4 fusion.37
  383.3 9.3 %fusion.14 = bf16[1,512,2048]{2,1,0:T(8,128)(2,1)} fusion(bf16[512,2048]{0,1:T(8,128)(2,1)S(1)} %bitcast.121, bf16[2048,2048]{1,0:T(8,128)(2,1)} %bitcast.8), kind=kOutput, calls=%fused_computation.32 | convolution fusion | flops 4296015872 | bytes 12582912 | tf_op jit(solution)/shard_map/dot_general | solution.py:130
  392.5 9.5 %all-gather.13.cloned.1.call-done = f32[4,16,128,128]{3,2,1,0:T(8,128)} async-done(((f32[1,16,128,128]{3,2,1,0:T(8,128)}), f32[4,16,128,128]{3,2,1,0:T(8,128)}) %all-gather.13.cloned.1.call-update) | async-done | bytes 4194320 | tf_op jit(solution)/shard_map/all_gather | solution.py:24
  402.1 5.5 %fusion.28 = bf16[16,128,128]{2,1,0:T(8,128)(2,1)S(1)} fusion(f32[4,16,128,128]{3,2,1,0:T(8,128)} %all-gather.13.cloned.1.call-done, f32[16,128,128]{2,1,0:T(8,128)S(1)} %copy-done.18, f32[64,128,128]{2,1,0:T(8,128)} %all-gather.21.cloned.1.call-done, f32[32,128,128]{2,1,0:T(8,128)} %all-gather.17.cloned.1.call-done, pred[]{:T(512)S(6)} %lt.37, pred[]{:T(512)S(6)} %lt.38, ...), kind=kLoop, calls=%fused_computation.50 | loop fusion | flops 5767168 | bytes 12058634 | tf_op jit(solution)/shard_map/convert_element_type | solution.py:141
  407.6 3.3 convolution_add_fusion
  411.0 5.6 %copy.74 = f32[1,512,2048]{2,1,0:T(8,128)} copy(f32[1,512,2048]{1,2,0:T(8,128)} %bitcast.116) | data formatting | bytes 8388608 | tf_op jit(solution)/shard_map/reshape | solution.py:148
  416.5 7.3 %fusion.6 = (bf16[1,512,2048]{2,1,0:T(8,128)(2,1)}, bf16[1,512,2048]{2,1,0:T(8,128)(2,1)}) fusion(f32[1,512,2048]{2,1,0:T(8,128)} %copy.69, bf16[1,512,2048]{2,1,0:T(8,128)(2,1)} %param.6, f32[1,512,2048]{2,1,0:T(8,128)} %copy.74, bf16[1,512,2048]{2,1,0:T(8,128)(2,1)S(1)} %copy-done.20), kind=kLoop, calls=%fused_computation.15 | loop fusion | flops 20971520 | bytes 16777216 | tf_op jit(solution)/shard_map/convert_element_type | solution.py:145
  423.8 60.6 %reduce-scatter.7.cloned.1.call-done = bf16[1,64,2048]{2,1,0:T(8,128)(2,1)} async-done(((bf16[16,64,2048]{2,1,0:T(8,128)(2,1)}), bf16[1,64,2048]{2,1,0:T(8,128)(2,1)}) %reduce-scatter.7.cloned.1.call-update) | async-done | bytes 262160
  484.4 4.8 all-to-all-start.1
  489.2 5.1 %add_convert_fusion = bf16[16,128,512]{2,1,0:T(8,128)(2,1)} fusion(f32[16,128,512]{2,1,0:T(8,128)} %fusion.39, bf16[16,128,128]{2,1,0:T(8,128)(2,1)S(1)} %copy-done.22, bf16[512,16,128]{2,0,1:T(8,128)(2,1)} %copy-done.9), kind=kOutput, calls=%fused_computation.24 | convolution fusion | flops 270532608 | bytes 8912896 | tf_op jit(solution)/shard_map/while/body/eval_jaxpr/jhd,hde->jhe/dot_general | solution.py:72
  494.3 3.9 copy.78
  (76 shorter events, 5.6 us)
Async XLA Ops:
  7.2 236.1 %copy-start = (bf16[1,512,2048]{2,1,0:T(8,128)(2,1)S(1)}, bf16[1,512,2048]{2,1,0:T(8,128)(2,1)}, u32[]{:S(2)}) copy-start(bf16[1,512,2048]{2,1,0:T(8,128)(2,1)} %param.9) | copy-start | bytes 6291460
  7.2 25.2 %all-gather.15.cloned.1.call-start = ((), (), s32[]{:S(2)}) async-start(), calls=%async_computation.7 | async-start | bytes 3145728 | tf_op jit(solution)/shard_map/all_gather | solution.py:24
  7.2 2.4 copy-start.19
  9.6 3.1 copy-start.12
  12.7 1.4 copy-start.9
  14.1 21.0 %copy-start.25 = (bf16[16,2048]{1,0:T(8,128)(2,1)S(1)}, bf16[16,2048]{1,0:T(8,128)(2,1)}, u32[]{:S(2)}) copy-start(bf16[16,2048]{1,0:T(8,128)(2,1)} %param.10) | copy-start | bytes 196612
  16.5 159.7 %all-gather.19.cloned.1.call-start = ((), (), s32[]{:S(2)}) async-start(), calls=%async_computation.9 | async-start | bytes 5242880 | tf_op jit(solution)/shard_map/all_gather | solution.py:24
  39.4 203.9 %all-to-all-start = ((bf16[128,16,2048]{2,1,0:T(8,128)(2,1)}), bf16[128,16,2048]{2,1,0:T(8,128)(2,1)}, u32[]{:S(2)}, u32[]{:S(2)}) async-start(bf16[128,16,2048]{2,1,0:T(8,128)(2,1)} %stack.2), calls=%async_computation | async-start | bytes 16777216 | tf_op jit(solution)/shard_map/all_to_all | solution.py:123
  49.3 179.4 %all-gather.11.cloned.1.call-start = ((), (), s32[]{:S(2)}) async-start(), calls=%async_computation.4 | async-start | bytes 5242880 | tf_op jit(solution)/shard_map/all_gather | solution.py:24
  179.7 96.9 %all-gather.17.cloned.1.call-start = ((), (), s32[]{:S(2)}) async-start(), calls=%async_computation.8 | async-start | bytes 3145728 | tf_op jit(solution)/shard_map/all_gather | solution.py:24
  183.3 3.1 copy-start.10
  185.0 1.3 copy-start.5
  186.3 6.0 %copy-start.13 = (bf16[64,8,16,128]{3,2,1,0:T(8,128)(2,1)S(1)}, bf16[64,8,16,128]{3,2,1,0:T(8,128)(2,1)}, u32[]{:S(2)}) copy-start(bf16[64,8,16,128]{3,2,1,0:T(8,128)(2,1)} %copy-done.12) | copy-start | bytes 6291460
  188.8 3.6 copy-start.4
  228.7 5.9 %copy-start.6 = (bf16[512,16,128]{2,0,1:T(8,128)(2,1)S(1)}, bf16[512,16,128]{2,0,1:T(8,128)(2,1)}, u32[]{:S(2)}) copy-start(bf16[512,16,128]{2,0,1:T(8,128)(2,1)} %copy-done.5) | copy-start | bytes 6291460
  228.7 6.2 %copy-start.16 = (f32[16,512,128]{1,2,0:T(8,128)S(1)}, f32[16,512,128]{1,2,0:T(8,128)}, u32[]{:S(2)}) copy-start(f32[16,512,128]{1,2,0:T(8,128)} %fusion.18) | copy-start | bytes 12582916
  237.7 5.6 %copy-start.26 = (f32[2048]{0:T(1024)S(1)}, f32[2048]{0:T(1024)}, u32[]{:S(2)}) copy-start(f32[2048]{0:T(1024)} %param.11) | copy-start | bytes 24580
  243.3 9.3 %copy-start.17 = (f32[512,2048]{1,0:T(8,128)S(1)}, f32[512,2048]{1,0:T(8,128)}, u32[]{:S(2)}) copy-start(f32[512,2048]{1,0:T(8,128)} %copy.64) | copy-start | bytes 12582916
  262.8 66.4 %all-gather.21.cloned.1.call-start = ((), (), s32[]{:S(2)}) async-start(), calls=%async_computation.10 | async-start | bytes 5242880 | tf_op jit(solution)/shard_map/all_gather | solution.py:24
  279.3 71.6 %reduce-scatter.5.cloned.1.call-start = ((), (), s32[]{:S(2)}) async-start(), calls=%async_computation.6 | async-start | bytes 12582912 | tf_op jit(solution)/shard_map/reduce_scatter | solution.py:45
  282.0 6.8 %copy-start.23 = (bf16[512,16,128]{0,2,1:T(8,128)(2,1)}, bf16[512,16,128]{0,2,1:T(8,128)(2,1)S(1)}, u32[]{:S(2)}) copy-start(bf16[512,16,128]{0,2,1:T(8,128)(2,1)S(1)} %multiply_convert_fusion) | copy-start | bytes 6291460
  297.8 53.2 %copy-start.8 = (bf16[512,2048]{0,1:T(8,128)(2,1)S(1)}, bf16[512,2048]{0,1:T(8,128)(2,1)}, u32[]{:S(2)}) copy-start(bf16[512,2048]{0,1:T(8,128)(2,1)} %copy.85) | copy-start | bytes 6291460
  297.8 104.3 %all-gather.13.cloned.1.call-start = ((), (), s32[]{:S(2)}) async-start(), calls=%async_computation.5 | async-start | bytes 5242880 | tf_op jit(solution)/shard_map/all_gather | solution.py:24
  332.6 151.8 %reduce-scatter.7.cloned.1.call-start = ((), (), s32[]{:S(2)}) async-start(), calls=%async_computation.11 | async-start | bytes 4456448
  350.9 4.6 copy-start.11
  355.6 4.9 copy-start.2
  371.1 7.7 %copy-start.3 = (bf16[16,512,512]{2,1,0:T(8,128)(2,1)S(1)}, bf16[16,512,512]{2,1,0:T(8,128)(2,1)}, u32[]{:S(2)}) copy-start(bf16[16,512,512]{2,1,0:T(8,128)(2,1)} %copy-done.2) | copy-start | bytes 25165828
  371.1 8.7 %copy-start.7 = (bf16[512,16,128]{2,0,1:T(8,128)(2,1)S(1)}, bf16[512,16,128]{2,0,1:T(8,128)(2,1)}, u32[]{:S(2)}) copy-start(bf16[512,16,128]{2,0,1:T(8,128)(2,1)} %copy-done.5) | copy-start | bytes 6291460
  379.8 3.4 copy-start.24
  383.3 18.8 %copy-start.18 = (f32[16,128,128]{2,1,0:T(8,128)S(1)}, f32[16,128,128]{2,1,0:T(8,128)}, u32[]{:S(2)}) copy-start(f32[16,128,128]{2,1,0:T(8,128)} %fusion.38) | copy-start | bytes 3145732
  392.5 15.1 %copy-start.14 = (bf16[64,8,16,128]{3,2,1,0:T(8,128)(2,1)S(1)}, bf16[64,8,16,128]{3,2,1,0:T(8,128)(2,1)}, u32[]{:S(2)}) copy-start(bf16[64,8,16,128]{3,2,1,0:T(8,128)(2,1)} %copy-done.12) | copy-start | bytes 6291460
  402.1 5.5 %copy-start.15 = (f32[16,128,512]{2,1,0:T(8,128)S(1)}, f32[16,128,512]{2,1,0:T(8,128)}, u32[]{:S(2)}) copy-start(f32[16,128,512]{2,1,0:T(8,128)} %fusion.37) | copy-start | bytes 12582916
  407.6 3.3 copy-start.21
  411.0 5.6 %copy-start.20 = (bf16[1,512,2048]{2,1,0:T(8,128)(2,1)S(1)}, bf16[1,512,2048]{2,1,0:T(8,128)(2,1)}, u32[]{:S(2)}) copy-start(bf16[1,512,2048]{2,1,0:T(8,128)(2,1)} %param.7) | copy-start | bytes 6291460
  416.5 72.7 %copy-start.22 = (bf16[16,128,128]{2,1,0:T(8,128)(2,1)S(1)}, bf16[16,128,128]{2,1,0:T(8,128)(2,1)}, u32[]{:S(2)}) copy-start(bf16[16,128,128]{2,1,0:T(8,128)(2,1)} %copy-done.21) | copy-start | bytes 1572868
  484.4 13.8 %all-to-all-start.1 = ((bf16[4,16,2048]{2,1,0:T(8,128)(2,1)}), bf16[4,16,2048]{2,1,0:T(8,128)(2,1)S(1)}, u32[]{:S(2)}, u32[]{:S(2)}) async-start(bf16[4,16,2048]{2,1,0:T(8,128)(2,1)} %bitcast.123), calls=%async_computation.2 | async-start | bytes 524288 | tf_op jit(solution)/shard_map/all_to_all | solution.py:51
  489.2 9.7 %copy-start.1 = (bf16[1,512,2048]{2,1,0:T(8,128)(2,1)S(1)}, bf16[1,512,2048]{2,1,0:T(8,128)(2,1)}, u32[]{:S(2)}) copy-start(bf16[1,512,2048]{2,1,0:T(8,128)(2,1)} %param.9) | copy-start | bytes 6291460
Sparse Core Ops, SparseCore 0:
  16.6 15.6 all-gather.14
  35.2 140.9 all-gather.18
  179.8 48.8 all-gather.10
  262.9 13.6 all-gather.16
  279.4 49.6 all-gather.20
  331.4 19.4 reduce-scatter.4
  352.5 49.4 all-gather.12
  405.4 78.9 reduce-scatter.6
